TPU v7x, 32 devices: a whole 2x2x4 slice. The times are simulated.
32 devices in a mesh: section: 4 (over x, core), mp: 8 (over z, y).
Axes of the slice: x: 2, y: 2, z: 4, core: 2. Of those that a mesh axis runs over, the one named last changes fastest.
Arguments:
- encoder_input: bfloat16 [576, 1024], P('section'), may hold values from -6 to 6
- input_gain: float32 [1024], replicated, may hold values from 0.1 to 1.9
- expand_weight: bfloat16 [1024, 8192], P(None, 'mp'), may hold values from -0.1875 to 0.1875
- reduce_weight: bfloat16 [8192, 1024], P('mp'), may hold values from -0.0625 to 0.0625
- final_gain: float32 [1024], replicated, may hold values from 0.1 to 1.9
- decoder_input: bfloat16 [1024, 1024], P('section'), may hold values from -6 to 6
- query_gain: float32 [1024], replicated, may hold values from 0.1 to 1.9
- query_weight: bfloat16 [1024, 2048], P(None, 'mp'), may hold values from -2 to 2
- key_weight: bfloat16 [1024, 2048], P(None, 'mp'), may hold values from -0.1875 to 0.1875
- value_weight: bfloat16 [1024, 2048], P(None, 'mp'), may hold values from -0.1875 to 0.1875
- mixing_weight: bfloat16 [2048, 1024], P('mp'), may hold values from -0.125 to 0.125
- output_gradient: bfloat16 [1024, 1024], P('section'), may hold values from -84 to 84
Outputs:
- memory: bfloat16 [576, 1024], P(('section', 'mp'))
- memory_gradient: bfloat16 [576, 1024], P(('section', 'mp'))
All inputs are finite; a program needn't handle non-finite values.
Results may differ from a plain program's by a relative error of at most 0.025.
The roundings to bfloat16 on the way count: a program that leaves them out, or rounds other values in their place, can miss the bound.
Values may be sent and summed in bfloat16 or wider, within the bound.
No kernel may reach another device: no remote copies, remote signals or barrier semaphores. Data moves between devices by JAX's collectives and lax.ppermute only.
A program may use at most 64 MiB of HBM per device.

v0:
```python
import jax
import jax.numpy as jnp
from jax import lax
from jax.sharding import PartitionSpec as P

DK = 128


def joined(x, axis, combine):
    everything = jax.tree.map(lambda part: lax.all_gather(part, axis), x)
    first = jax.tree.map(lambda part: part[0], everything)

    def lap(k, so_far):
        return combine(so_far, jax.tree.map(lambda part: part[k], everything))

    return lax.fori_loop(1, lax.axis_size(axis), lap, first)


def norm_rows(rows, gain):
    values = rows.astype(jnp.float32)
    return values * lax.rsqrt(jnp.mean(values * values, axis=-1, keepdims=True) + 1e-06) * gain


def combine(first, second):
    top = jnp.maximum(first[0], second[0])
    left = jnp.exp(first[0] - top)
    right = jnp.exp(second[0] - top)
    return (top, first[1] * left + second[1] * right, first[2] * left + second[2] * right)


def body(
    encoder_input,
    input_gain,
    expand_weight,
    reduce_weight,
    final_gain,
    decoder_input,
    query_gain,
    query_weight,
    key_weight,
    value_weight,
    mixing_weight,
    output_gradient,
):
    scale = DK ** (-0.5)
    heads = key_weight.shape[1] // DK
    width = heads * DK
    normed = norm_rows(encoder_input, input_gain).astype(jnp.bfloat16)
    hidden = jnp.maximum(
        jnp.dot(normed, expand_weight, preferred_element_type=jnp.float32), 0.0
    ).astype(jnp.bfloat16)
    partial_value = jnp.dot(hidden, reduce_weight, preferred_element_type=jnp.float32)
    share = encoder_input.shape[0] // lax.axis_size("mp")
    offset = lax.axis_index("mp") * share
    summed = lax.psum(partial_value, "mp")
    memory = norm_rows(encoder_input.astype(jnp.float32) + summed, final_gain).astype(jnp.bfloat16)
    memory_own = lax.dynamic_slice_in_dim(memory, offset, share, 0)
    keys = jnp.dot(memory, key_weight, preferred_element_type=jnp.float32).astype(jnp.bfloat16)
    values = jnp.dot(memory, value_weight, preferred_element_type=jnp.float32).astype(jnp.bfloat16)
    dec_normed = norm_rows(decoder_input, query_gain).astype(jnp.bfloat16)
    queries = jnp.dot(dec_normed, query_weight, preferred_element_type=jnp.float32).astype(
        jnp.bfloat16
    )
    head_grad = jnp.einsum(
        "qd,id->qi", output_gradient, mixing_weight, preferred_element_type=jnp.float32
    ).astype(jnp.bfloat16)
    all_queries, all_grads = (
        lax.all_gather(queries, "section", axis=0, tiled=True),
        lax.all_gather(head_grad, "section", axis=0, tiled=True),
    )
    query_heads = all_queries.reshape(all_queries.shape[0], heads, DK)
    grad_heads = all_grads.reshape(all_grads.shape[0], heads, DK)
    key_heads = keys.reshape(keys.shape[0], heads, DK)
    value_heads = values.reshape(values.shape[0], heads, DK)
    scores = (
        jnp.einsum("qhd,khd->hqk", query_heads, key_heads, preferred_element_type=jnp.float32)
        * scale
    )
    local_top = jnp.max(scores, axis=-1)
    weights = jnp.exp(scores - local_top[..., None])
    prob_grad = jnp.einsum(
        "qhd,khd->hqk", grad_heads, value_heads, preferred_element_type=jnp.float32
    )
    top, total, numer = joined(
        (local_top, jnp.sum(weights, axis=-1), jnp.sum(weights * prob_grad, axis=-1)),
        "section",
        combine,
    )
    probs = jnp.exp(scores - top[..., None]) / total[..., None]
    delta = (numer / total)[..., None]
    score_grad = (probs * (prob_grad - delta) * scale).astype(jnp.bfloat16)
    key_grad = (
        jnp.einsum("hqk,qhd->khd", score_grad, query_heads, preferred_element_type=jnp.float32)
        .reshape(keys.shape[0], width)
        .astype(jnp.bfloat16)
    )
    value_grad = (
        jnp.einsum(
            "hqk,qhd->khd",
            probs.astype(jnp.bfloat16),
            grad_heads,
            preferred_element_type=jnp.float32,
        )
        .reshape(keys.shape[0], width)
        .astype(jnp.bfloat16)
    )
    first = jnp.einsum("ki,di->kd", key_grad, key_weight, preferred_element_type=jnp.float32)
    second = jnp.einsum("ki,di->kd", value_grad, value_weight, preferred_element_type=jnp.float32)
    gradient = lax.psum_scatter(first + second, "mp", scatter_dimension=0, tiled=True)
    return (memory_own, gradient.astype(jnp.bfloat16))


def solution(mesh):
    in_specs = (
        P("section", None),
        P(),
        P(None, "mp"),
        P("mp", None),
        P(),
        P("section", None),
        P(),
        P(None, "mp"),
        P(None, "mp"),
        P(None, "mp"),
        P("mp", None),
        P("section", None),
    )
    out_specs = (P(("section", "mp"), None), P(("section", "mp"), None))
    return jax.shard_map(body, mesh=mesh, in_specs=in_specs, out_specs=out_specs, check_vma=False)
```

profile of v0, /device:TPU:0, one launch (start us, length us, event | category | flops | bytes accessed | tf_op | source)
XLA Modules:
  0.0 153.6 jit_solution(9564051884883702727)
XLA Ops:
  7.2 1.2 fusion.14
  8.5 0.4 copy-done
  8.9 3.4 %fusion.5 = f32[144,1024]{1,0:T(8,128)} fusion(bf16[1024,1024]{1,0:T(8,128)(2,1)S(1)} %copy-done, bf16[1024,1024]{1,0:T(8,128)(2,1)} %param.16, bf16[144,1024]{1,0:T(8,128)(2,1)} %param.14, f32[1024]{0:T(1024)} %param.15, f32[144]{0:T(256)S(1)} %add_rsqrt_fusion.2), kind=kOutput, calls=%fused_computation.18 | convolution fusion | flops 604864512 | bytes 5083712 | tf_op jit(solution)/shard_map/dot_general | solution.py:52
  12.5 0.6 dynamic-slice.4
  13.8 1.5 convolution_convert_fusion.1
  15.3 9.2 %all_gather.24 = bf16[1024,256]{1,0:T(8,128)(2,1)} all-gather(bf16[256,256]{1,0:T(8,128)(2,1)S(1)} %convolution_convert_fusion.1), channel_id=1, replica_groups=mesh['section'=4,'mp'=8] {'section'}, dimensions={0}, use_global_device_ids=true | all-gather | bytes 655360 | tf_op jit(solution)/shard_map/all_gather | solution.py:68
  24.5 0.3 convolution_convert_fusion
  24.8 7.7 %all_gather.29 = bf16[1024,256]{1,0:T(8,128)(2,1)} all-gather(bf16[256,256]{1,0:T(8,128)(2,1)S(1)} %convolution_convert_fusion), channel_id=1, replica_groups=mesh['section'=4,'mp'=8] {'section'}, dimensions={0}, use_global_device_ids=true | all-gather | bytes 655360 | tf_op jit(solution)/shard_map/all_gather | solution.py:69
  32.6 55.9 %all-reduce.4.cloned.1.call-done = f32[144,1024]{1,0:T(8,128)} async-done(((f32[144,1024]{1,0:T(8,128)}), f32[144,1024]{1,0:T(8,128)}) %all-reduce.4.cloned.1.call-update) | async-done | bytes 589840 | tf_op jit(solution)/shard_map/psum | solution.py:55
  88.4 1.3 multiply_reduce_fusion.1
  90.2 0.4 copy-done.2
  91.5 5.2 %all-gather.3 = f32[4,2,1024]{2,1,0:T(2,128)S(1)} all-gather(f32[1,2,1024]{2,1,0:T(2,128)S(1)} %bitcast.101), channel_id=2, replica_groups=mesh['section'=4,'mp'=8] {'section'}, dimensions={0}, use_global_device_ids=true | all-gather | bytes 40960 | tf_op jit(solution)/shard_map/all_gather | solution.py:10
  96.7 1.4 multiply_reduce_fusion
  98.0 5.2 %all-gather.4 = f32[4,2,1024]{2,1,0:T(2,128)S(1)} all-gather(f32[1,2,1024]{2,1,0:T(2,128)S(1)} %bitcast.103), channel_id=3, replica_groups=mesh['section'=4,'mp'=8] {'section'}, dimensions={0}, use_global_device_ids=true | all-gather | bytes 40960 | tf_op jit(solution)/shard_map/all_gather | solution.py:10
  103.2 5.2 %all-gather.5 = f32[4,2,1024]{2,1,0:T(2,128)S(1)} all-gather(f32[1,2,1024]{2,1,0:T(2,128)S(1)} %bitcast.102), channel_id=4, replica_groups=mesh['section'=4,'mp'=8] {'section'}, dimensions={0}, use_global_device_ids=true | all-gather | bytes 40960 | tf_op jit(solution)/shard_map/all_gather | solution.py:10
  108.7 1.5 fusion.9
  110.3 0.5 fusion.8
  110.7 0.6 copy-done.9
  111.6 0.7 copy-done.5
  112.7 25.6 %fusion = f32[24,1024]{1,0:T(8,128)S(1)} fusion(f32[144,1024]{1,0:T(8,128)S(1)} %convolution_add_fusion), kind=kCustom, calls=%all-reduce-scatter | all-reduce-scatter fusion | flops 196609 | bytes 688640
  138.3 1.4 collective-permute-start.1
  139.7 4.3 %collective-permute-start = (bf16[24,1024]{1,0:T(8,128)(2,1)S(1)}, bf16[24,1024]{1,0:T(8,128)(2,1)S(1)}, u32[]{:S(2)}, u32[]{:S(2)}) collective-permute-start(bf16[24,1024]{1,0:T(8,128)(2,1)S(1)} %convert.6), channel_id=1, source_target_pairs={{0,1},{1,2},{2,3},{3,4},{4,5},{5,6},{6,7},{8,9},{9,10},{10,11},{11... | collective-permute-start | bytes 147464
  144.1 1.5 constant_dynamic-slice_fusion
  146.1 0.6 dynamic-slice_convert_fusion
  (63 shorter events, 3.3 us)
Async XLA Ops:
  7.2 1.7 %copy-start = (bf16[1024,1024]{1,0:T(8,128)(2,1)S(1)}, bf16[1024,1024]{1,0:T(8,128)(2,1)}, u32[]{:S(2)}) copy-start(bf16[1024,1024]{1,0:T(8,128)(2,1)} %param.17) | copy-start | bytes 6291460
  7.2 81.2 %all-reduce.4.cloned.1.call-start = ((), (), s32[]{:S(2)}) async-start(), calls=%async_computation | async-start | bytes 1179648 | tf_op jit(solution)/shard_map/psum | solution.py:55
  8.8 3.5 %copy-start.12 = (bf16[256,1024]{1,0:T(8,128)(2,1)S(1)}, bf16[256,1024]{1,0:T(8,128)(2,1)}, u32[]{:S(2)}) copy-start(bf16[256,1024]{1,0:T(8,128)(2,1)} %param.19) | copy-start | bytes 1572868
  8.9 3.7 %copy-start.16 = (u32[32]{0:T(128)S(1)}, u32[32]{0:T(128)}, u32[]{:S(2)}) copy-start(u32[32]{0:T(128)} %constant.64) | copy-start | bytes 388
  8.9 4.9 %copy-start.17 = (f32[1024]{0:T(1024)S(1)}, f32[1024]{0:T(1024)}, u32[]{:S(2)}) copy-start(f32[1024]{0:T(1024)} %param.20) | copy-start | bytes 12292
  12.5 12.0 %copy-start.13 = (bf16[256,1024]{1,0:T(8,128)(2,1)S(1)}, bf16[256,1024]{1,0:T(8,128)(2,1)}, u32[]{:S(2)}) copy-start(bf16[256,1024]{1,0:T(8,128)(2,1)} %param.25) | copy-start | bytes 1572868
  13.8 10.7 %copy-start.14 = (bf16[256,1024]{1,0:T(8,128)(2,1)S(1)}, bf16[256,1024]{1,0:T(8,128)(2,1)}, u32[]{:S(2)}) copy-start(bf16[256,1024]{1,0:T(8,128)(2,1)} %param.24) | copy-start | bytes 1572868
  15.2 73.2 %copy-start.1 = (bf16[144,1024]{1,0:T(8,128)(2,1)S(1)}, bf16[144,1024]{1,0:T(8,128)(2,1)}, u32[]{:S(2)}) copy-start(bf16[144,1024]{1,0:T(8,128)(2,1)} %param.14) | copy-start | bytes 884740
  24.5 65.3 %copy-start.15 = (f32[1024]{0:T(1024)S(1)}, f32[1024]{0:T(1024)}, u32[]{:S(2)}) copy-start(f32[1024]{0:T(1024)} %param.18) | copy-start | bytes 12292
  88.4 1.3 copy-start.3
  88.4 1.5 copy-start.8
  89.7 1.1 copy-start.4
  89.9 0.7 copy-start.2
  89.9 1.2 copy-start.6
  90.8 5.8 %copy-start.10 = (bf16[1024,256]{1,0:T(8,128)(2,1)S(1)}, bf16[1024,256]{1,0:T(8,128)(2,1)}, u32[]{:S(2)}) copy-start(bf16[1024,256]{1,0:T(8,128)(2,1)} %all_gather.29) | copy-start | bytes 1572868
  108.7 1.5 copy-start.7
  108.7 1.6 %copy-start.11 = (f32[2,1024,144]{1,2,0:T(8,128)S(1)}, f32[2,1024,144]{1,2,0:T(8,128)}, u32[]{:S(2)}) copy-start(f32[2,1024,144]{1,2,0:T(8,128)} %get-tuple-element.203) | copy-start | bytes 3538948
  110.3 1.0 copy-start.9
  111.3 1.0 copy-start.5
  138.3 7.2 %collective-permute-start.1 = (bf16[18,1024]{1,0:T(8,128)(2,1)S(1)}, bf16[18,1024]{1,0:T(8,128)(2,1)S(1)}, u32[]{:S(2)}, u32[]{:S(2)}) collective-permute-start(bf16[18,1024]{1,0:T(8,128)(2,1)S(1)} %slice.21), channel_id=1, source_target_pairs={{0,2},{1,3},{2,4},{3,5},{4,6},{5,7},{8,10},{9,11},{10,12},{11,13},... | collective-permute-start | bytes 110600
  139.7 6.0 %collective-permute-start = (bf16[24,1024]{1,0:T(8,128)(2,1)S(1)}, bf16[24,1024]{1,0:T(8,128)(2,1)S(1)}, u32[]{:S(2)}, u32[]{:S(2)}) collective-permute-start(bf16[24,1024]{1,0:T(8,128)(2,1)S(1)} %convert.6), channel_id=1, source_target_pairs={{0,1},{1,2},{2,3},{3,4},{4,5},{5,6},{6,7},{8,9},{9,10},{10,11},{11... | collective-permute-start | bytes 147464
Sparse Core Ops, SparseCore 0:
  12.4 75.9 all-reduce.3
where the time goes:
time: 154 us
  blocking collectives  58.1 us (38%)
  waiting for transfers between devices  56.1 us (36%)
  between operations  15 us (10%)
  matrix products  9.97 us (6%)
  starting transfers between devices  5.77 us (4%)
  local copies, waits for them, and re-layouts  5.49 us (4%)
  other arithmetic  3.11 us (2%)
    psum x1, waiting for transfers between devices, body(): summed = lax.psum(partial_value, 'mp')  55.9 us
    unnamed x1, blocking collectives  25.6 us
    all_gather x3, blocking collectives, joined(): everything = jax.tree.map(lambda part: lax.all_gather(part, axis), x)  15.5 us
    all_gather x1, blocking collectives, body(): lax.all_gather(queries, 'section', axis=0, tiled=True)  9.22 us
    all_gather x1, blocking collectives, body(): lax.all_gather(head_grad, 'section', axis=0, tiled=True)  7.73 us
    unnamed x2, starting transfers between devices  5.74 us
    dot_general x1, matrix products, body(): jnp.dot(hidden, reduce_weight, preferred_element_type=jnp.float32)  3.41 us
    unnamed x39, local copies, waits for them, and re-layouts  3.35 us
  transfers between devices with their start and end apart: 3, of which 2 were waited for; matrix products, arithmetic and copies ran while one was open for 3% of the time, Pallas kernels for 0%

commit v1 on v0

--- a/solution.py
+++ b/solution.py
@@ -52,7 +52,9 @@
     partial_value = jnp.dot(hidden, reduce_weight, preferred_element_type=jnp.float32)
     share = encoder_input.shape[0] // lax.axis_size("mp")
     offset = lax.axis_index("mp") * share
-    summed = lax.psum(partial_value, "mp")
+    summed = partial_value
+    for hop in (1, 2, 4):
+        summed = summed + lax.ppermute(summed, "mp", [(dev, dev ^ hop) for dev in range(8)])
     memory = norm_rows(encoder_input.astype(jnp.float32) + summed, final_gain).astype(jnp.bfloat16)
     memory_own = lax.dynamic_slice_in_dim(memory, offset, share, 0)
     keys = jnp.dot(memory, key_weight, preferred_element_type=jnp.float32).astype(jnp.bfloat16)

time: 154 us -> 121 us (0.79)
  waiting for transfers between devices: 56.1 us -> 34.3 us
  between operations: 15 us -> 1.61 us
  starting transfers between devices: 5.77 us -> 12.9 us
  blocking collectives: 58.1 us -> 56.1 us
  matrix products: 9.97 us -> 8.01 us
    psum x1 -> x0, waiting for transfers between devices: 55.9 us -> none  [body(): summed = lax.psum(partial_value, 'mp')]
    ppermute x0 -> x3, waiting for transfers between devices: none -> 34 us  [body(): lax.ppermute(summed, 'mp', [(dev, dev ^ hop) for dev in range(8)])]
    ppermute x0 -> x3, starting transfers between devices: none -> 7.51 us  [body(): lax.ppermute(summed, 'mp', [(dev, dev ^ hop) for dev in range(8)])]
    all_gather x1, blocking collectives: 9.22 us -> 7.14 us  [body(): lax.all_gather(queries, 'section', axis=0, tiled=True)]
  transfers between devices with their start and end apart: 3 -> 5, of which waited for: 2 -> 4; matrix products, arithmetic and copies ran while one was open for 3% -> 2% of each run, Pallas kernels for 0% -> 0%
where the time goes in v1:
time: 121 us
  blocking collectives  56.1 us (46%)
  waiting for transfers between devices  34.3 us (28%)
  starting transfers between devices  12.9 us (11%)
  matrix products  8.01 us (7%)
  local copies, waits for them, and re-layouts  5.73 us (5%)
  other arithmetic  2.14 us (2%)
  between operations  1.61 us (1%)
    ppermute x3, waiting for transfers between devices, body(): lax.ppermute(summed, 'mp', [(dev, dev ^ hop) for dev in range(8)])  34 us
    unnamed x1, blocking collectives  26.1 us
    all_gather x3, blocking collectives, joined(): everything = jax.tree.map(lambda part: lax.all_gather(part, axis), x)  15.5 us
    ppermute x3, starting transfers between devices, body(): lax.ppermute(summed, 'mp', [(dev, dev ^ hop) for dev in range(8)])  7.51 us
    all_gather x1, blocking collectives, body(): lax.all_gather(head_grad, 'section', axis=0, tiled=True)  7.28 us
    all_gather x1, blocking collectives, body(): lax.all_gather(queries, 'section', axis=0, tiled=True)  7.14 us
    unnamed x2, starting transfers between devices  5.43 us
    unnamed x39, local copies, waits for them, and re-layouts  3.59 us
  transfers between devices with their start and end apart: 5, of which 4 were waited for; matrix products, arithmetic and copies ran while one was open for 2% of the time, Pallas kernels for 0%

profile of v1, /device:TPU:0, one launch (start us, length us, event | category | flops | bytes accessed | tf_op | source)
XLA Modules:
  0.0 120.9 jit_solution(1433297650220362936)
XLA Ops:
  0.6 1.3 %fusion.14 = f32[144]{0:T(256)S(1)} fusion(bf16[144,1024]{1,0:T(8,128)(2,1)} %param.14), kind=kLoop, calls=%fused_computation.36 | loop fusion | flops 442224 | bytes 295488 | tf_op jit(solution)/shard_map/reduce_sum | solution.py:21
  2.3 2.6 %fusion.5 = f32[144,1024]{1,0:T(8,128)S(1)} fusion(bf16[1024,1024]{1,0:T(8,128)(2,1)S(1)} %copy-done, bf16[1024,1024]{1,0:T(8,128)(2,1)} %param.16, bf16[144,1024]{1,0:T(8,128)(2,1)} %param.14, f32[1024]{0:T(1024)} %param.15, f32[144]{0:T(256)S(1)} %add_rsqrt_fusion.2), kind=kOutput, calls=%fused_computation.18 | convolution fusion | flops 604864512 | bytes 5083712 | tf_op jit(solution)/shard_map/dot_general | solution.py:52
  4.9 3.1 %collective-permute-start = (f32[144,1024]{1,0:T(8,128)S(1)}, f32[144,1024]{1,0:T(8,128)S(1)}, u32[]{:S(2)}, u32[]{:S(2)}) collective-permute-start(f32[144,1024]{1,0:T(8,128)S(1)} %fusion.5), channel_id=1, source_target_pairs={{0,1},{1,0},{2,3},{3,2},{4,5},{5,4},{6,7},{7,6},{8,9},{9,8},{10,11... | collective-permute-start | bytes 1769480 | tf_op jit(solution)/shard_map/ppermute | solution.py:57
  8.0 0.6 dynamic-slice.4
  9.2 12.1 %collective-permute-done = f32[144,1024]{1,0:T(8,128)S(1)} collective-permute-done((f32[144,1024]{1,0:T(8,128)S(1)}, f32[144,1024]{1,0:T(8,128)S(1)}, u32[]{:S(2)}, u32[]{:S(2)}) %collective-permute-start) | collective-permute-done | bytes 589856 | tf_op jit(solution)/shard_map/ppermute | solution.py:57
  21.4 1.9 %collective-permute-start.1 = (f32[144,1024]{1,0:T(8,128)S(1)}, f32[144,1024]{1,0:T(8,128)S(1)}, u32[]{:S(2)}, u32[]{:S(2)}) collective-permute-start(f32[144,1024]{1,0:T(8,128)S(1)} %add.103), channel_id=1, source_target_pairs={{0,2},{1,3},{2,0},{3,1},{4,6},{5,7},{6,4},{7,5},{8,10},{9,11},{10,... | collective-permute-start | bytes 1769480 | tf_op jit(solution)/shard_map/ppermute | solution.py:57
  23.8 12.1 %collective-permute-done.1 = f32[144,1024]{1,0:T(8,128)S(1)} collective-permute-done((f32[144,1024]{1,0:T(8,128)S(1)}, f32[144,1024]{1,0:T(8,128)S(1)}, u32[]{:S(2)}, u32[]{:S(2)}) %collective-permute-start.1) | collective-permute-done | bytes 589856 | tf_op jit(solution)/shard_map/ppermute | solution.py:57
  36.0 2.6 %collective-permute-start.2 = (f32[144,1024]{1,0:T(8,128)S(1)}, f32[144,1024]{1,0:T(8,128)S(1)}, u32[]{:S(2)}, u32[]{:S(2)}) collective-permute-start(f32[144,1024]{1,0:T(8,128)S(1)} %add.104), channel_id=1, source_target_pairs={{0,4},{1,5},{2,6},{3,7},{4,0},{5,1},{6,2},{7,3},{8,12},{9,13},{10,... | collective-permute-start | bytes 1769480 | tf_op jit(solution)/shard_map/ppermute | solution.py:57
  38.6 7.1 %all_gather.24 = bf16[1024,256]{1,0:T(8,128)(2,1)S(1)} all-gather(bf16[256,256]{1,0:T(8,128)(2,1)S(1)} %convolution_convert_fusion.1), channel_id=1, replica_groups=mesh['section'=4,'mp'=8] {'section'}, dimensions={0}, use_global_device_ids=true | all-gather | bytes 655360 | tf_op jit(solution)/shard_map/all_gather | solution.py:70
  46.1 7.3 %all_gather.29 = bf16[1024,256]{1,0:T(8,128)(2,1)S(1)} all-gather(bf16[256,256]{1,0:T(8,128)(2,1)S(1)} %convolution_convert_fusion), channel_id=1, replica_groups=mesh['section'=4,'mp'=8] {'section'}, dimensions={0}, use_global_device_ids=true | all-gather | bytes 655360 | tf_op jit(solution)/shard_map/all_gather | solution.py:71
  53.4 9.9 %collective-permute-done.2 = f32[144,1024]{1,0:T(8,128)S(1)} collective-permute-done((f32[144,1024]{1,0:T(8,128)S(1)}, f32[144,1024]{1,0:T(8,128)S(1)}, u32[]{:S(2)}, u32[]{:S(2)}) %collective-permute-start.2) | collective-permute-done | bytes 589856 | tf_op jit(solution)/shard_map/ppermute | solution.py:57
  63.6 0.9 copy-done.7
  65.3 5.2 %all-gather.3 = f32[4,2,1024]{2,1,0:T(2,128)S(1)} all-gather(f32[1,2,1024]{2,1,0:T(2,128)S(1)} %bitcast.101), channel_id=2, replica_groups=mesh['section'=4,'mp'=8] {'section'}, dimensions={0}, use_global_device_ids=true | all-gather | bytes 40960 | tf_op jit(solution)/shard_map/all_gather | solution.py:10
  70.5 1.4 %multiply_reduce_fusion = (f32[2,1024]{1,0:T(2,128)S(1)}, f32[2,1024]{1,0:T(2,128)S(1)}, f32[2,1024,144]{1,2,0:T(8,128)}) fusion(f32[2,1024,144]{1,2,0:T(8,128)S(1)} %get-tuple-element.202, f32[2,1024]{1,0:T(2,128)S(1)} %get-tuple-element.201, bf16[18,2,8,128]{3,2,1,0:T(8,128)(2,1)S(1)} %fusion.7, bf16[1024,256]{1,0:T(8,128)(2,1)S(1)} %all_gather.29), kind=kOutput, calls=%fused_computation.16 | convolution fusion | flops 76673024 | bytes 2981888 | tf_op jit(solution)/shard_map/qhd,khd->hqk/dot_general | solution.py:83
  71.9 5.2 %all-gather.4 = f32[4,2,1024]{2,1,0:T(2,128)S(1)} all-gather(f32[1,2,1024]{2,1,0:T(2,128)S(1)} %bitcast.103), channel_id=3, replica_groups=mesh['section'=4,'mp'=8] {'section'}, dimensions={0}, use_global_device_ids=true | all-gather | bytes 40960 | tf_op jit(solution)/shard_map/all_gather | solution.py:10
  77.1 5.2 %all-gather.5 = f32[4,2,1024]{2,1,0:T(2,128)S(1)} all-gather(f32[1,2,1024]{2,1,0:T(2,128)S(1)} %bitcast.102), channel_id=4, replica_groups=mesh['section'=4,'mp'=8] {'section'}, dimensions={0}, use_global_device_ids=true | all-gather | bytes 40960 | tf_op jit(solution)/shard_map/all_gather | solution.py:10
  82.6 1.5 %fusion.9 = bf16[2,18,8,128]{3,2,1,0:T(8,128)(2,1)S(1)} fusion(f32[2,1024,144]{1,2,0:T(8,128)S(1)} %get-tuple-element.202, f32[2,1024]{1,0:T(2,128)S(1)} %get-tuple-element.181, f32[2,1024]{1,0:T(2,128)S(1)} %get-tuple-element.180, bf16[1024,256]{1,0:T(8,128)(2,1)} %copy-done.9), kind=kOutput, calls=%fused_computation.28 | convolution fusion | flops 76419072 | bytes 1794048 | tf_op jit(solution)/shard_map/hqk,qhd->khd/dot_general | solution.py:100
  84.6 0.6 copy-done.8
  85.5 0.7 copy-done.4
  86.6 26.1 %fusion = f32[24,1024]{1,0:T(8,128)S(1)} fusion(f32[144,1024]{1,0:T(8,128)S(1)} %convolution_add_fusion), kind=kCustom, calls=%all-reduce-scatter | all-reduce-scatter fusion | flops 196609 | bytes 688640
  112.7 1.3 %collective-permute-start.4 = (bf16[18,1024]{1,0:T(8,128)(2,1)S(1)}, bf16[18,1024]{1,0:T(8,128)(2,1)S(1)}, u32[]{:S(2)}, u32[]{:S(2)}) collective-permute-start(bf16[18,1024]{1,0:T(8,128)(2,1)S(1)} %slice.21), channel_id=1, source_target_pairs={{0,2},{1,3},{2,4},{3,5},{4,6},{5,7},{8,10},{9,11},{10,12},{11,13},... | collective-permute-start | bytes 110600
  114.0 4.1 %collective-permute-start.3 = (bf16[24,1024]{1,0:T(8,128)(2,1)S(1)}, bf16[24,1024]{1,0:T(8,128)(2,1)S(1)}, u32[]{:S(2)}, u32[]{:S(2)}) collective-permute-start(bf16[24,1024]{1,0:T(8,128)(2,1)S(1)} %convert.6), channel_id=1, source_target_pairs={{0,1},{1,2},{2,3},{3,4},{4,5},{5,6},{6,7},{8,9},{9,10},{10,11},{11... | collective-permute-start | bytes 147464
  118.2 1.5 %constant_dynamic-slice_fusion = bf16[18,1024]{1,0:T(8,128)(2,1)} fusion(bf16[144,1024]{1,0:T(8,128)(2,1)} %copy-done.2, s32[]{:T(128)S(6)} %select_n.15), kind=kLoop, calls=%fused_computation.74 | loop fusion | bytes 73732 | tf_op jit(solution)/shard_map/dynamic_slice | solution.py:59
  120.2 0.6 dynamic-slice_convert_fusion
  (68 shorter events, 4.9 us)
Async XLA Ops:
  0.6 1.7 %copy-start = (bf16[1024,1024]{1,0:T(8,128)(2,1)S(1)}, bf16[1024,1024]{1,0:T(8,128)(2,1)}, u32[]{:S(2)}) copy-start(bf16[1024,1024]{1,0:T(8,128)(2,1)} %param.17) | copy-start | bytes 6291460
  2.3 5.6 %copy-start.15 = (u32[32]{0:T(128)S(1)}, u32[32]{0:T(128)}, u32[]{:S(2)}) copy-start(u32[32]{0:T(128)} %constant.64) | copy-start | bytes 388
  4.9 18.5 %copy-start.17 = (f32[1024]{0:T(1024)S(1)}, f32[1024]{0:T(1024)}, u32[]{:S(2)}) copy-start(f32[1024]{0:T(1024)} %param.20) | copy-start | bytes 12292
  4.9 16.4 %collective-permute-start = (f32[144,1024]{1,0:T(8,128)S(1)}, f32[144,1024]{1,0:T(8,128)S(1)}, u32[]{:S(2)}, u32[]{:S(2)}) collective-permute-start(f32[144,1024]{1,0:T(8,128)S(1)} %fusion.5), channel_id=1, source_target_pairs={{0,1},{1,0},{2,3},{3,2},{4,5},{5,4},{6,7},{7,6},{8,9},{9,8},{10,11... | collective-permute-start | bytes 1769480 | tf_op jit(solution)/shard_map/ppermute | solution.py:57
  9.2 14.0 %copy-start.11 = (bf16[256,1024]{1,0:T(8,128)(2,1)S(1)}, bf16[256,1024]{1,0:T(8,128)(2,1)}, u32[]{:S(2)}) copy-start(bf16[256,1024]{1,0:T(8,128)(2,1)} %param.19) | copy-start | bytes 1572868
  9.2 14.2 %copy-start.16 = (bf16[1024,256]{1,0:T(8,128)(2,1)S(1)}, bf16[1024,256]{1,0:T(8,128)(2,1)}, u32[]{:S(2)}) copy-start(bf16[1024,256]{1,0:T(8,128)(2,1)} %param.21) | copy-start | bytes 1572868
  21.4 14.6 %collective-permute-start.1 = (f32[144,1024]{1,0:T(8,128)S(1)}, f32[144,1024]{1,0:T(8,128)S(1)}, u32[]{:S(2)}, u32[]{:S(2)}) collective-permute-start(f32[144,1024]{1,0:T(8,128)S(1)} %add.103), channel_id=1, source_target_pairs={{0,2},{1,3},{2,0},{3,1},{4,6},{5,7},{6,4},{7,5},{8,10},{9,11},{10,... | collective-permute-start | bytes 1769480 | tf_op jit(solution)/shard_map/ppermute | solution.py:57
  23.8 21.9 %copy-start.12 = (bf16[256,1024]{1,0:T(8,128)(2,1)S(1)}, bf16[256,1024]{1,0:T(8,128)(2,1)}, u32[]{:S(2)}) copy-start(bf16[256,1024]{1,0:T(8,128)(2,1)} %param.25) | copy-start | bytes 1572868
  23.8 21.9 %copy-start.13 = (bf16[256,1024]{1,0:T(8,128)(2,1)S(1)}, bf16[256,1024]{1,0:T(8,128)(2,1)}, u32[]{:S(2)}) copy-start(bf16[256,1024]{1,0:T(8,128)(2,1)} %param.24) | copy-start | bytes 1572868
  36.0 27.3 %copy-start.1 = (bf16[144,1024]{1,0:T(8,128)(2,1)S(1)}, bf16[144,1024]{1,0:T(8,128)(2,1)}, u32[]{:S(2)}) copy-start(bf16[144,1024]{1,0:T(8,128)(2,1)} %param.14) | copy-start | bytes 884740
  36.0 27.2 %collective-permute-start.2 = (f32[144,1024]{1,0:T(8,128)S(1)}, f32[144,1024]{1,0:T(8,128)S(1)}, u32[]{:S(2)}, u32[]{:S(2)}) collective-permute-start(f32[144,1024]{1,0:T(8,128)S(1)} %add.104), channel_id=1, source_target_pairs={{0,4},{1,5},{2,6},{3,7},{4,0},{5,1},{6,2},{7,3},{8,12},{9,13},{10,... | collective-permute-start | bytes 1769480 | tf_op jit(solution)/shard_map/ppermute | solution.py:57
  45.7 19.2 %copy-start.5 = (bf16[1024,256]{1,0:T(8,128)(2,1)}, bf16[1024,256]{1,0:T(8,128)(2,1)S(1)}, u32[]{:S(2)}) copy-start(bf16[1024,256]{1,0:T(8,128)(2,1)S(1)} %all_gather.24) | copy-start | bytes 1572868
  46.1 17.4 %copy-start.14 = (f32[1024]{0:T(1024)S(1)}, f32[1024]{0:T(1024)}, u32[]{:S(2)}) copy-start(f32[1024]{0:T(1024)} %param.18) | copy-start | bytes 12292
  53.4 17.2 %copy-start.9 = (bf16[1024,256]{1,0:T(8,128)(2,1)}, bf16[1024,256]{1,0:T(8,128)(2,1)S(1)}, u32[]{:S(2)}) copy-start(bf16[1024,256]{1,0:T(8,128)(2,1)S(1)} %all_gather.29) | copy-start | bytes 1572868
  63.4 1.0 copy-start.7
  63.5 1.3 %copy-start.3 = (bf16[1024,256]{1,0:T(8,128)(2,1)S(1)}, bf16[1024,256]{1,0:T(8,128)(2,1)}, u32[]{:S(2)}) copy-start(bf16[1024,256]{1,0:T(8,128)(2,1)} %param.23) | copy-start | bytes 1572868
  64.5 0.9 copy-start.2
  82.6 1.5 %copy-start.6 = (bf16[1024,256]{1,0:T(8,128)(2,1)S(1)}, bf16[1024,256]{1,0:T(8,128)(2,1)}, u32[]{:S(2)}) copy-start(bf16[1024,256]{1,0:T(8,128)(2,1)} %copy-done.5) | copy-start | bytes 1572868
  82.6 1.6 %copy-start.10 = (f32[2,1024,144]{1,2,0:T(8,128)S(1)}, f32[2,1024,144]{1,2,0:T(8,128)}, u32[]{:S(2)}) copy-start(f32[2,1024,144]{1,2,0:T(8,128)} %get-tuple-element.203) | copy-start | bytes 3538948
  84.1 1.0 copy-start.8
  85.2 1.0 copy-start.4
  112.7 6.9 %collective-permute-start.4 = (bf16[18,1024]{1,0:T(8,128)(2,1)S(1)}, bf16[18,1024]{1,0:T(8,128)(2,1)S(1)}, u32[]{:S(2)}, u32[]{:S(2)}) collective-permute-start(bf16[18,1024]{1,0:T(8,128)(2,1)S(1)} %slice.21), channel_id=1, source_target_pairs={{0,2},{1,3},{2,4},{3,5},{4,6},{5,7},{8,10},{9,11},{10,12},{11,13},... | collective-permute-start | bytes 110600
  114.0 5.9 %collective-permute-start.3 = (bf16[24,1024]{1,0:T(8,128)(2,1)S(1)}, bf16[24,1024]{1,0:T(8,128)(2,1)S(1)}, u32[]{:S(2)}, u32[]{:S(2)}) collective-permute-start(bf16[24,1024]{1,0:T(8,128)(2,1)S(1)} %convert.6), channel_id=1, source_target_pairs={{0,1},{1,2},{2,3},{3,4},{4,5},{5,6},{6,7},{8,9},{9,10},{10,11},{11... | collective-permute-start | bytes 147464
